TPU v7x, 32 devices: a whole 2x2x4 slice. The times are simulated.
32 devices in a mesh: sub: 4 (over x, core), gx: 4 (over z), gy: 2 (over y).
Axes of the slice: x: 2, y: 2, z: 4, core: 2. Of those that a mesh axis runs over, the one named last changes fastest.
Arguments:
- state: float32 [4, 256, 512], P(None, ('sub', 'gx'), 'gy'), may hold values from -4 to 4
- damping: float32 [4, 256, 512], P(None, ('sub', 'gx'), 'gy'), may hold values from 0.005 to 0.1
- weights: float32 [4], replicated, may hold values from 0.5 to 1.5
Outputs:
- combined: float32 [4, 256, 512], P(None, ('sub', 'gx'), 'gy')
- column_error: float32 [4, 512], P(None, 'gy')
All inputs are finite; a program needn't handle non-finite values.
Results may differ from a plain program's by a relative error of at most 0.0003.
Values sent between devices are 32-bit elements; how exact they have to be, the bound alone decides.
A program may use at most 64 MiB of HBM per device.

v0:
```python
import jax
import jax.numpy as jnp
from jax import lax
from jax.sharding import PartitionSpec as P

KRYLOV = 12
SUBSTEPS = 4


dt_total = 4.0
sound_sq = 1.0
buoyancy_sq = 0.5
norm_eps = 1e-06
taylor_degree = 12
squarings = 8


def padded(cells, sides, width):
    for axis, dim in sides:
        count = lax.axis_size(axis)
        ends = count - 1
        head = lax.slice_in_dim(cells, 0, width, axis=dim)
        tail = lax.slice_in_dim(cells, cells.shape[dim] - width, cells.shape[dim], axis=dim)
        cells = jnp.concatenate(
            [
                lax.ppermute(tail, axis, [(i, (i + 1) % count) for i in range(ends)]),
                cells,
                lax.ppermute(head, axis, [((i + 1) % count, i) for i in range(ends)]),
            ],
            axis=dim,
        )
    return cells


def wave(field):
    row_pair = jnp.stack([field[0], field[3]])
    column_pair = jnp.stack([field[1], field[3]])
    rows_padded = padded(row_pair, ((("sub", "gx"), 1),), 1)
    columns_padded = padded(column_pair, (("gy", 2),), 1)
    rise_x = 0.5 * (rows_padded[1, 2:, :] - rows_padded[1, :-2, :])
    rise_y = 0.5 * (columns_padded[1, :, 2:] - columns_padded[1, :, :-2])
    spread = 0.5 * (rows_padded[0, 2:, :] - rows_padded[0, :-2, :]) + 0.5 * (
        columns_padded[0, :, 2:] - columns_padded[0, :, :-2]
    )
    return jnp.stack([-rise_x, -rise_y + field[2], -buoyancy_sq * field[1], -sound_sq * spread])


def phi_first(hessenberg):
    extent = hessenberg.shape[0]
    augmented = jnp.zeros((extent + 1, extent + 1), jnp.float32)
    augmented = augmented.at[:extent, :extent].set(hessenberg).at[0, extent].set(1.0)
    scaled = augmented / 2.0**squarings
    result = jnp.eye(extent + 1, dtype=jnp.float32)
    power_term = result
    for degree in range(1, taylor_degree + 1):
        power_term = jnp.dot(power_term, scaled, precision=lax.Precision.HIGHEST) / degree
        result = result + power_term
    for repeat in range(squarings):
        result = jnp.dot(result, result, precision=lax.Precision.HIGHEST)
    return result[:extent, extent]


def arnoldi(start, stiffness):
    shape = start.shape
    basis = jnp.zeros((KRYLOV + 1, start.size), jnp.float32).at[0].set(start.reshape(-1))
    hessenberg = jnp.zeros((KRYLOV + 1, KRYLOV), jnp.float32)
    for column in range(KRYLOV):
        current = basis[column].reshape(shape)
        image = (dt_total * (wave(current) - stiffness * current)).reshape(-1)
        partial_value = jnp.dot(basis[: column + 1], image, precision=lax.Precision.HIGHEST)
        products, squared = lax.psum((partial_value, jnp.sum(image * image)), ("sub", "gx", "gy"))
        image = image - jnp.dot(products, basis[: column + 1], precision=lax.Precision.HIGHEST)
        length = jnp.sqrt(jnp.maximum(squared - jnp.sum(products * products), 0.0) + norm_eps)
        hessenberg = (
            hessenberg.at[: column + 1, column].set(products).at[column + 1, column].set(length)
        )
        basis = basis.at[column + 1].set(image / length)
    return (basis, hessenberg)


def shards(state, damping, weights):
    stiffness = 3.0 * damping * state * state
    forcing = wave(state) - damping * state * state * state
    beta_norm = jnp.sqrt(lax.psum(jnp.sum(forcing * forcing), ("sub", "gx", "gy")) + norm_eps)
    basis, hessenberg = arnoldi(forcing / beta_norm, stiffness)
    mixing = jnp.zeros((KRYLOV,), jnp.float32)
    highest = jnp.zeros((), jnp.float32)
    for member in range(SUBSTEPS):
        fraction = (member + 1) / SUBSTEPS
        factor = dt_total * fraction
        coefficients = phi_first(fraction * hessenberg[:KRYLOV])
        mixing = mixing + weights[member] * factor * beta_norm * coefficients
        estimate = (
            factor
            * beta_norm
            * fraction
            * hessenberg[KRYLOV, KRYLOV - 1]
            * jnp.abs(coefficients[KRYLOV - 1])
        )
        highest = jnp.maximum(highest, estimate)
    increment = jnp.dot(mixing, basis[:KRYLOV], precision=lax.Precision.HIGHEST)
    combined = state + increment.reshape(state.shape)
    local_peak = highest * jnp.max(jnp.abs(basis[KRYLOV].reshape(state.shape)), axis=1)
    column_error = lax.pmax(local_peak, ("sub", "gx"))
    return (combined, column_error)


def solution(mesh):
    return jax.shard_map(
        shards,
        mesh=mesh,
        in_specs=(P(None, ("sub", "gx"), "gy"), P(None, ("sub", "gx"), "gy"), P()),
        out_specs=(P(None, ("sub", "gx"), "gy"), P(None, "gy")),
        check_vma=False,
    )
```

profile of v0, /device:TPU:0, one launch (start us, length us, event | category | flops | bytes accessed | tf_op | source)
XLA Modules:
  0.0 885.9 jit_solution(2977581656855364826)
XLA Ops:
  2.7 4.9 collective-permute-start.3
  23.8 5.2 collective-permute-start.1
  33.7 41.0 %psum.175 = f32[]{:T(128)} all-reduce(f32[]{:T(128)} %get-tuple-element.640), channel_id=1, replica_groups=mesh['sub'=4,'gx'=4,'gy'=2] {'sub','gx','gy'}, use_global_device_ids=true, to_apply=%region_1.0 | all-reduce | flops 1 | bytes 8 | tf_op jit(solution)/shard_map/psum | solution.py:84
  77.1 4.7 collective-permute-start.5
  89.8 42.5 %all-reduce.17 = (f32[]{:T(128)}, f32[1]{0:T(128)}) all-reduce(f32[]{:T(128)} %get-tuple-element.587, f32[1]{0:T(128)} %bitcast.1), channel_id=1, replica_groups=mesh['sub'=4,'gx'=4,'gy'=2] {'sub','gx','gy'}, use_global_device_ids=true, to_apply=%region_4.0 | all-reduce | flops 2 | bytes 16 | tf_op jit(solution)/shard_map/psum | solution.py:71
  136.6 4.5 collective-permute-start.9
  142.5 4.5 collective-permute-start.11
  150.5 41.8 %all-reduce.16 = (f32[2]{0:T(128)S(1)}, f32[]{:T(128)}) all-reduce(f32[2]{0:T(128)S(1)} %convolution_bitcast_fusion.10, f32[]{:T(128)} %get-tuple-element.636), channel_id=1, replica_groups=mesh['sub'=4,'gx'=4,'gy'=2] {'sub','gx','gy'}, use_global_device_ids=true, to_apply=%region_6.0 | all-reduce | flops 3 | bytes 24 | tf_op jit(solution)/shard_map/psum | solution.py:71
  197.9 4.7 collective-permute-start.13
  204.5 4.5 collective-permute-start.15
  213.2 41.8 %all-reduce.15 = (f32[3]{0:T(128)S(1)}, f32[]{:T(128)}) all-reduce(f32[3]{0:T(128)S(1)} %convolution_bitcast_fusion.9, f32[]{:T(128)} %get-tuple-element.634), channel_id=1, replica_groups=mesh['sub'=4,'gx'=4,'gy'=2] {'sub','gx','gy'}, use_global_device_ids=true, to_apply=%region_11.0 | all-reduce | flops 4 | bytes 32 | tf_op jit(solution)/shard_map/psum | solution.py:71
  260.5 4.5 collective-permute-start.17
  267.0 4.5 collective-permute-start.19
  275.9 41.0 %all-reduce.14 = (f32[4]{0:T(128)S(1)}, f32[]{:T(128)}) all-reduce(f32[4]{0:T(128)S(1)} %convolution_bitcast_fusion.8, f32[]{:T(128)} %get-tuple-element.632), channel_id=1, replica_groups=mesh['sub'=4,'gx'=4,'gy'=2] {'sub','gx','gy'}, use_global_device_ids=true, to_apply=%region_16.0 | all-reduce | flops 5 | bytes 40 | tf_op jit(solution)/shard_map/psum | solution.py:71
  322.4 4.7 collective-permute-start.21
  329.1 4.5 collective-permute-start.23
  337.8 41.8 %all-reduce.13 = (f32[5]{0:T(128)S(1)}, f32[]{:T(128)}) all-reduce(f32[5]{0:T(128)S(1)} %convolution_bitcast_fusion.7, f32[]{:T(128)} %get-tuple-element.630), channel_id=1, replica_groups=mesh['sub'=4,'gx'=4,'gy'=2] {'sub','gx','gy'}, use_global_device_ids=true, to_apply=%region_21.0 | all-reduce | flops 6 | bytes 48 | tf_op jit(solution)/shard_map/psum | solution.py:71
  385.0 4.5 collective-permute-start.25
  400.2 41.1 %all-reduce.12 = (f32[6]{0:T(128)S(1)}, f32[]{:T(128)}) all-reduce(f32[6]{0:T(128)S(1)} %convolution_bitcast_fusion.6, f32[]{:T(128)} %get-tuple-element.628), channel_id=1, replica_groups=mesh['sub'=4,'gx'=4,'gy'=2] {'sub','gx','gy'}, use_global_device_ids=true, to_apply=%region_26.0 | all-reduce | flops 7 | bytes 56 | tf_op jit(solution)/shard_map/psum | solution.py:71
  446.9 4.7 collective-permute-start.29
  462.3 42.2 %all-reduce.11 = (f32[7]{0:T(128)S(1)}, f32[]{:T(128)}) all-reduce(f32[7]{0:T(128)S(1)} %convolution_bitcast_fusion.5, f32[]{:T(128)} %get-tuple-element.626), channel_id=1, replica_groups=mesh['sub'=4,'gx'=4,'gy'=2] {'sub','gx','gy'}, use_global_device_ids=true, to_apply=%region_31.0 | all-reduce | flops 8 | bytes 64 | tf_op jit(solution)/shard_map/psum | solution.py:71
  510.0 4.5 collective-permute-start.33
  525.3 41.1 %all-reduce.10 = (f32[8]{0:T(128)S(1)}, f32[]{:T(128)}) all-reduce(f32[8]{0:T(128)S(1)} %convolution_bitcast_fusion.4, f32[]{:T(128)} %get-tuple-element.624), channel_id=1, replica_groups=mesh['sub'=4,'gx'=4,'gy'=2] {'sub','gx','gy'}, use_global_device_ids=true, to_apply=%region_36.0 | all-reduce | flops 9 | bytes 72 | tf_op jit(solution)/shard_map/psum | solution.py:71
  571.9 4.7 collective-permute-start.37
  587.3 41.8 %all-reduce.9 = (f32[9]{0:T(128)S(1)}, f32[]{:T(128)}) all-reduce(f32[9]{0:T(128)S(1)} %convolution_bitcast_fusion.3, f32[]{:T(128)} %get-tuple-element.622), channel_id=1, replica_groups=mesh['sub'=4,'gx'=4,'gy'=2] {'sub','gx','gy'}, use_global_device_ids=true, to_apply=%region_41.0 | all-reduce | flops 10 | bytes 80 | tf_op jit(solution)/shard_map/psum | solution.py:71
  634.7 4.5 collective-permute-start.41
  650.0 41.3 %all-reduce.8 = (f32[10]{0:T(128)S(1)}, f32[]{:T(128)}) all-reduce(f32[10]{0:T(128)S(1)} %convolution_bitcast_fusion.2, f32[]{:T(128)} %get-tuple-element.620), channel_id=1, replica_groups=mesh['sub'=4,'gx'=4,'gy'=2] {'sub','gx','gy'}, use_global_device_ids=true, to_apply=%region_46.0 | all-reduce | flops 11 | bytes 88 | tf_op jit(solution)/shard_map/psum | solution.py:71
  696.9 4.7 collective-permute-start.45
  712.4 41.8 %all-reduce.7 = (f32[11]{0:T(128)S(1)}, f32[]{:T(128)}) all-reduce(f32[11]{0:T(128)S(1)} %convolution_bitcast_fusion.1, f32[]{:T(128)} %get-tuple-element.618), channel_id=1, replica_groups=mesh['sub'=4,'gx'=4,'gy'=2] {'sub','gx','gy'}, use_global_device_ids=true, to_apply=%region_51.0 | all-reduce | flops 12 | bytes 96 | tf_op jit(solution)/shard_map/psum | solution.py:71
  759.7 4.5 collective-permute-start.49
  775.4 40.7 %all-reduce.6 = (f32[12]{0:T(128)S(1)}, f32[]{:T(128)}) all-reduce(f32[12]{0:T(128)S(1)} %convolution_bitcast_fusion, f32[]{:T(128)} %get-tuple-element.616), channel_id=1, replica_groups=mesh['sub'=4,'gx'=4,'gy'=2] {'sub','gx','gy'}, use_global_device_ids=true, to_apply=%region_56.0 | all-reduce | flops 13 | bytes 104 | tf_op jit(solution)/shard_map/psum | solution.py:71
  851.6 32.4 %pmax.7 = f32[4,256]{1,0:T(4,128)} all-reduce(f32[4,256]{1,0:T(4,128)S(1)} %broadcast_multiply_fusion.68), channel_id=1, replica_groups=mesh['sub'=4,'gx'=4,'gy'=2] {'sub','gx'}, use_global_device_ids=true, to_apply=%region_62.0 | all-reduce | flops 1024 | bytes 8192 | tf_op jit(solution)/shard_map/pmax | solution.py:104
  (527 shorter events, 204.2 us)
Async XLA Ops:
  1.4 20.9 %collective-permute-start.2 = (f32[2,16,1]{2,1,0:T(8,128)S(1)}, f32[2,16,1]{2,1,0:T(8,128)S(1)}, u32[]{:S(2)}, u32[]{:S(2)}) collective-permute-start(f32[2,16,1]{2,1,0:T(8,128)S(1)} %get-tuple-element.735), channel_id=1, source_target_pairs={{1,0},{3,2},{5,4},{7,6},{9,8},{11,10},{13,12},{15,14},{17,16},{19,... | collective-permute-start | bytes 392 | tf_op jit(solution)/shard_map/ppermute | solution.py:28
  2.7 19.7 %collective-permute-start.3 = (f32[2,16,1]{2,1,0:T(8,128)S(1)}, f32[2,16,1]{2,1,0:T(8,128)S(1)}, u32[]{:S(2)}, u32[]{:S(2)}) collective-permute-start(f32[2,16,1]{2,1,0:T(8,128)S(1)} %get-tuple-element.736), channel_id=1, source_target_pairs={{0,1},{2,3},{4,5},{6,7},{8,9},{10,11},{12,13},{14,15},{16,17},{18,... | collective-permute-start | bytes 392 | tf_op jit(solution)/shard_map/ppermute | solution.py:26
  75.8 13.3 %collective-permute-start.4 = (f32[2,1,256]{2,1,0:T(1,128)S(1)}, f32[2,1,256]{2,1,0:T(1,128)S(1)}, u32[]{:S(2)}, u32[]{:S(2)}) collective-permute-start(f32[2,1,256]{2,1,0:T(1,128)S(1)} %get-tuple-element.729), channel_id=1, source_target_pairs={{2,0},{4,2},{6,4},{8,6},{10,8},{12,10},{14,12},{16,14},{18,16},{20... | collective-permute-start | bytes 6152 | tf_op jit(solution)/shard_map/ppermute | solution.py:28
  195.3 15.9 %collective-permute-start.14 = (f32[2,16,1]{2,1,0:T(8,128)S(1)}, f32[2,16,1]{2,1,0:T(8,128)S(1)}, u32[]{:S(2)}, u32[]{:S(2)}) collective-permute-start(f32[2,16,1]{2,1,0:T(8,128)S(1)} %get-tuple-element.723), channel_id=1, source_target_pairs={{1,0},{3,2},{5,4},{7,6},{9,8},{11,10},{13,12},{15,14},{17,16},{19,... | collective-permute-start | bytes 392 | tf_op jit(solution)/shard_map/ppermute | solution.py:28
  196.6 14.6 %collective-permute-start.12 = (f32[2,1,256]{2,1,0:T(1,128)S(1)}, f32[2,1,256]{2,1,0:T(1,128)S(1)}, u32[]{:S(2)}, u32[]{:S(2)}) collective-permute-start(f32[2,1,256]{2,1,0:T(1,128)S(1)} %get-tuple-element.721), channel_id=1, source_target_pairs={{2,0},{4,2},{6,4},{8,6},{10,8},{12,10},{14,12},{16,14},{18,16},{20... | collective-permute-start | bytes 6152 | tf_op jit(solution)/shard_map/ppermute | solution.py:28
  197.9 13.3 %collective-permute-start.13 = (f32[2,1,256]{2,1,0:T(1,128)S(1)}, f32[2,1,256]{2,1,0:T(1,128)S(1)}, u32[]{:S(2)}, u32[]{:S(2)}) collective-permute-start(f32[2,1,256]{2,1,0:T(1,128)S(1)} %get-tuple-element.722), channel_id=1, source_target_pairs={{0,2},{2,4},{4,6},{6,8},{8,10},{10,12},{12,14},{14,16},{16,18},{18... | collective-permute-start | bytes 6152 | tf_op jit(solution)/shard_map/ppermute | solution.py:26
  257.9 15.9 %collective-permute-start.18 = (f32[2,16,1]{2,1,0:T(8,128)S(1)}, f32[2,16,1]{2,1,0:T(8,128)S(1)}, u32[]{:S(2)}, u32[]{:S(2)}) collective-permute-start(f32[2,16,1]{2,1,0:T(8,128)S(1)} %get-tuple-element.719), channel_id=1, source_target_pairs={{1,0},{3,2},{5,4},{7,6},{9,8},{11,10},{13,12},{15,14},{17,16},{19,... | collective-permute-start | bytes 392 | tf_op jit(solution)/shard_map/ppermute | solution.py:28
  259.2 14.6 %collective-permute-start.16 = (f32[2,1,256]{2,1,0:T(1,128)S(1)}, f32[2,1,256]{2,1,0:T(1,128)S(1)}, u32[]{:S(2)}, u32[]{:S(2)}) collective-permute-start(f32[2,1,256]{2,1,0:T(1,128)S(1)} %get-tuple-element.717), channel_id=1, source_target_pairs={{2,0},{4,2},{6,4},{8,6},{10,8},{12,10},{14,12},{16,14},{18,16},{20... | collective-permute-start | bytes 6152 | tf_op jit(solution)/shard_map/ppermute | solution.py:28
  260.5 13.4 %collective-permute-start.17 = (f32[2,1,256]{2,1,0:T(1,128)S(1)}, f32[2,1,256]{2,1,0:T(1,128)S(1)}, u32[]{:S(2)}, u32[]{:S(2)}) collective-permute-start(f32[2,1,256]{2,1,0:T(1,128)S(1)} %get-tuple-element.718), channel_id=1, source_target_pairs={{0,2},{2,4},{4,6},{6,8},{8,10},{10,12},{12,14},{14,16},{16,18},{18... | collective-permute-start | bytes 6152 | tf_op jit(solution)/shard_map/ppermute | solution.py:26
  319.7 16.0 %collective-permute-start.22 = (f32[2,16,1]{2,1,0:T(8,128)S(1)}, f32[2,16,1]{2,1,0:T(8,128)S(1)}, u32[]{:S(2)}, u32[]{:S(2)}) collective-permute-start(f32[2,16,1]{2,1,0:T(8,128)S(1)} %get-tuple-element.715), channel_id=1, source_target_pairs={{1,0},{3,2},{5,4},{7,6},{9,8},{11,10},{13,12},{15,14},{17,16},{19,... | collective-permute-start | bytes 392 | tf_op jit(solution)/shard_map/ppermute | solution.py:28
  321.1 14.7 %collective-permute-start.20 = (f32[2,1,256]{2,1,0:T(1,128)S(1)}, f32[2,1,256]{2,1,0:T(1,128)S(1)}, u32[]{:S(2)}, u32[]{:S(2)}) collective-permute-start(f32[2,1,256]{2,1,0:T(1,128)S(1)} %get-tuple-element.713), channel_id=1, source_target_pairs={{2,0},{4,2},{6,4},{8,6},{10,8},{12,10},{14,12},{16,14},{18,16},{20... | collective-permute-start | bytes 6152 | tf_op jit(solution)/shard_map/ppermute | solution.py:28
  322.4 13.4 %collective-permute-start.21 = (f32[2,1,256]{2,1,0:T(1,128)S(1)}, f32[2,1,256]{2,1,0:T(1,128)S(1)}, u32[]{:S(2)}, u32[]{:S(2)}) collective-permute-start(f32[2,1,256]{2,1,0:T(1,128)S(1)} %get-tuple-element.714), channel_id=1, source_target_pairs={{0,2},{2,4},{4,6},{6,8},{8,10},{10,12},{12,14},{14,16},{16,18},{18... | collective-permute-start | bytes 6152 | tf_op jit(solution)/shard_map/ppermute | solution.py:26
  382.4 15.7 %collective-permute-start.26 = (f32[2,16,1]{2,1,0:T(8,128)S(1)}, f32[2,16,1]{2,1,0:T(8,128)S(1)}, u32[]{:S(2)}, u32[]{:S(2)}) collective-permute-start(f32[2,16,1]{2,1,0:T(8,128)S(1)} %get-tuple-element.711), channel_id=1, source_target_pairs={{1,0},{3,2},{5,4},{7,6},{9,8},{11,10},{13,12},{15,14},{17,16},{19,... | collective-permute-start | bytes 392 | tf_op jit(solution)/shard_map/ppermute | solution.py:28
  383.7 14.4 %collective-permute-start.24 = (f32[2,1,256]{2,1,0:T(1,128)S(1)}, f32[2,1,256]{2,1,0:T(1,128)S(1)}, u32[]{:S(2)}, u32[]{:S(2)}) collective-permute-start(f32[2,1,256]{2,1,0:T(1,128)S(1)} %get-tuple-element.709), channel_id=1, source_target_pairs={{2,0},{4,2},{6,4},{8,6},{10,8},{12,10},{14,12},{16,14},{18,16},{20... | collective-permute-start | bytes 6152 | tf_op jit(solution)/shard_map/ppermute | solution.py:28
  444.3 16.0 %collective-permute-start.30 = (f32[2,16,1]{2,1,0:T(8,128)S(1)}, f32[2,16,1]{2,1,0:T(8,128)S(1)}, u32[]{:S(2)}, u32[]{:S(2)}) collective-permute-start(f32[2,16,1]{2,1,0:T(8,128)S(1)} %get-tuple-element.707), channel_id=1, source_target_pairs={{1,0},{3,2},{5,4},{7,6},{9,8},{11,10},{13,12},{15,14},{17,16},{19,... | collective-permute-start | bytes 392 | tf_op jit(solution)/shard_map/ppermute | solution.py:28
  445.6 14.7 %collective-permute-start.28 = (f32[2,1,256]{2,1,0:T(1,128)S(1)}, f32[2,1,256]{2,1,0:T(1,128)S(1)}, u32[]{:S(2)}, u32[]{:S(2)}) collective-permute-start(f32[2,1,256]{2,1,0:T(1,128)S(1)} %get-tuple-element.705), channel_id=1, source_target_pairs={{2,0},{4,2},{6,4},{8,6},{10,8},{12,10},{14,12},{16,14},{18,16},{20... | collective-permute-start | bytes 6152 | tf_op jit(solution)/shard_map/ppermute | solution.py:28
  446.9 13.4 %collective-permute-start.29 = (f32[2,1,256]{2,1,0:T(1,128)S(1)}, f32[2,1,256]{2,1,0:T(1,128)S(1)}, u32[]{:S(2)}, u32[]{:S(2)}) collective-permute-start(f32[2,1,256]{2,1,0:T(1,128)S(1)} %get-tuple-element.706), channel_id=1, source_target_pairs={{0,2},{2,4},{4,6},{6,8},{8,10},{10,12},{12,14},{14,16},{16,18},{18... | collective-permute-start | bytes 6152 | tf_op jit(solution)/shard_map/ppermute | solution.py:26
  507.4 15.9 %collective-permute-start.34 = (f32[2,16,1]{2,1,0:T(8,128)S(1)}, f32[2,16,1]{2,1,0:T(8,128)S(1)}, u32[]{:S(2)}, u32[]{:S(2)}) collective-permute-start(f32[2,16,1]{2,1,0:T(8,128)S(1)} %get-tuple-element.703), channel_id=1, source_target_pairs={{1,0},{3,2},{5,4},{7,6},{9,8},{11,10},{13,12},{15,14},{17,16},{19,... | collective-permute-start | bytes 392 | tf_op jit(solution)/shard_map/ppermute | solution.py:28
  508.7 14.6 %collective-permute-start.32 = (f32[2,1,256]{2,1,0:T(1,128)S(1)}, f32[2,1,256]{2,1,0:T(1,128)S(1)}, u32[]{:S(2)}, u32[]{:S(2)}) collective-permute-start(f32[2,1,256]{2,1,0:T(1,128)S(1)} %get-tuple-element.701), channel_id=1, source_target_pairs={{2,0},{4,2},{6,4},{8,6},{10,8},{12,10},{14,12},{16,14},{18,16},{20... | collective-permute-start | bytes 6152 | tf_op jit(solution)/shard_map/ppermute | solution.py:28
  510.0 13.3 %collective-permute-start.33 = (f32[2,1,256]{2,1,0:T(1,128)S(1)}, f32[2,1,256]{2,1,0:T(1,128)S(1)}, u32[]{:S(2)}, u32[]{:S(2)}) collective-permute-start(f32[2,1,256]{2,1,0:T(1,128)S(1)} %get-tuple-element.702), channel_id=1, source_target_pairs={{0,2},{2,4},{4,6},{6,8},{8,10},{10,12},{12,14},{14,16},{16,18},{18... | collective-permute-start | bytes 6152 | tf_op jit(solution)/shard_map/ppermute | solution.py:26
  569.3 15.8 %collective-permute-start.38 = (f32[2,16,1]{2,1,0:T(8,128)S(1)}, f32[2,16,1]{2,1,0:T(8,128)S(1)}, u32[]{:S(2)}, u32[]{:S(2)}) collective-permute-start(f32[2,16,1]{2,1,0:T(8,128)S(1)} %get-tuple-element.699), channel_id=1, source_target_pairs={{1,0},{3,2},{5,4},{7,6},{9,8},{11,10},{13,12},{15,14},{17,16},{19,... | collective-permute-start | bytes 392 | tf_op jit(solution)/shard_map/ppermute | solution.py:28
  570.6 14.5 %collective-permute-start.36 = (f32[2,1,256]{2,1,0:T(1,128)S(1)}, f32[2,1,256]{2,1,0:T(1,128)S(1)}, u32[]{:S(2)}, u32[]{:S(2)}) collective-permute-start(f32[2,1,256]{2,1,0:T(1,128)S(1)} %get-tuple-element.697), channel_id=1, source_target_pairs={{2,0},{4,2},{6,4},{8,6},{10,8},{12,10},{14,12},{16,14},{18,16},{20... | collective-permute-start | bytes 6152 | tf_op jit(solution)/shard_map/ppermute | solution.py:28
  571.9 13.2 %collective-permute-start.37 = (f32[2,1,256]{2,1,0:T(1,128)S(1)}, f32[2,1,256]{2,1,0:T(1,128)S(1)}, u32[]{:S(2)}, u32[]{:S(2)}) collective-permute-start(f32[2,1,256]{2,1,0:T(1,128)S(1)} %get-tuple-element.698), channel_id=1, source_target_pairs={{0,2},{2,4},{4,6},{6,8},{8,10},{10,12},{12,14},{14,16},{16,18},{18... | collective-permute-start | bytes 6152 | tf_op jit(solution)/shard_map/ppermute | solution.py:26
  632.1 15.8 %collective-permute-start.42 = (f32[2,16,1]{2,1,0:T(8,128)S(1)}, f32[2,16,1]{2,1,0:T(8,128)S(1)}, u32[]{:S(2)}, u32[]{:S(2)}) collective-permute-start(f32[2,16,1]{2,1,0:T(8,128)S(1)} %get-tuple-element.695), channel_id=1, source_target_pairs={{1,0},{3,2},{5,4},{7,6},{9,8},{11,10},{13,12},{15,14},{17,16},{19,... | collective-permute-start | bytes 392 | tf_op jit(solution)/shard_map/ppermute | solution.py:28
  633.4 14.5 %collective-permute-start.40 = (f32[2,1,256]{2,1,0:T(1,128)S(1)}, f32[2,1,256]{2,1,0:T(1,128)S(1)}, u32[]{:S(2)}, u32[]{:S(2)}) collective-permute-start(f32[2,1,256]{2,1,0:T(1,128)S(1)} %get-tuple-element.693), channel_id=1, source_target_pairs={{2,0},{4,2},{6,4},{8,6},{10,8},{12,10},{14,12},{16,14},{18,16},{20... | collective-permute-start | bytes 6152 | tf_op jit(solution)/shard_map/ppermute | solution.py:28
  634.7 13.2 %collective-permute-start.41 = (f32[2,1,256]{2,1,0:T(1,128)S(1)}, f32[2,1,256]{2,1,0:T(1,128)S(1)}, u32[]{:S(2)}, u32[]{:S(2)}) collective-permute-start(f32[2,1,256]{2,1,0:T(1,128)S(1)} %get-tuple-element.694), channel_id=1, source_target_pairs={{0,2},{2,4},{4,6},{6,8},{8,10},{10,12},{12,14},{14,16},{16,18},{18... | collective-permute-start | bytes 6152 | tf_op jit(solution)/shard_map/ppermute | solution.py:26
  694.3 15.9 %collective-permute-start.46 = (f32[2,16,1]{2,1,0:T(8,128)S(1)}, f32[2,16,1]{2,1,0:T(8,128)S(1)}, u32[]{:S(2)}, u32[]{:S(2)}) collective-permute-start(f32[2,16,1]{2,1,0:T(8,128)S(1)} %get-tuple-element.691), channel_id=1, source_target_pairs={{1,0},{3,2},{5,4},{7,6},{9,8},{11,10},{13,12},{15,14},{17,16},{19,... | collective-permute-start | bytes 392 | tf_op jit(solution)/shard_map/ppermute | solution.py:28
  695.6 14.7 %collective-permute-start.44 = (f32[2,1,256]{2,1,0:T(1,128)S(1)}, f32[2,1,256]{2,1,0:T(1,128)S(1)}, u32[]{:S(2)}, u32[]{:S(2)}) collective-permute-start(f32[2,1,256]{2,1,0:T(1,128)S(1)} %get-tuple-element.689), channel_id=1, source_target_pairs={{2,0},{4,2},{6,4},{8,6},{10,8},{12,10},{14,12},{16,14},{18,16},{20... | collective-permute-start | bytes 6152 | tf_op jit(solution)/shard_map/ppermute | solution.py:28
  696.9 13.4 %collective-permute-start.45 = (f32[2,1,256]{2,1,0:T(1,128)S(1)}, f32[2,1,256]{2,1,0:T(1,128)S(1)}, u32[]{:S(2)}, u32[]{:S(2)}) collective-permute-start(f32[2,1,256]{2,1,0:T(1,128)S(1)} %get-tuple-element.690), channel_id=1, source_target_pairs={{0,2},{2,4},{4,6},{6,8},{8,10},{10,12},{12,14},{14,16},{16,18},{18... | collective-permute-start | bytes 6152 | tf_op jit(solution)/shard_map/ppermute | solution.py:26
  757.1 16.1 %collective-permute-start.50 = (f32[2,16,1]{2,1,0:T(8,128)S(1)}, f32[2,16,1]{2,1,0:T(8,128)S(1)}, u32[]{:S(2)}, u32[]{:S(2)}) collective-permute-start(f32[2,16,1]{2,1,0:T(8,128)S(1)} %get-tuple-element.687), channel_id=1, source_target_pairs={{1,0},{3,2},{5,4},{7,6},{9,8},{11,10},{13,12},{15,14},{17,16},{19,... | collective-permute-start | bytes 392 | tf_op jit(solution)/shard_map/ppermute | solution.py:28
  758.4 14.9 %collective-permute-start.48 = (f32[2,1,256]{2,1,0:T(1,128)S(1)}, f32[2,1,256]{2,1,0:T(1,128)S(1)}, u32[]{:S(2)}, u32[]{:S(2)}) collective-permute-start(f32[2,1,256]{2,1,0:T(1,128)S(1)} %get-tuple-element.685), channel_id=1, source_target_pairs={{2,0},{4,2},{6,4},{8,6},{10,8},{12,10},{14,12},{16,14},{18,16},{20... | collective-permute-start | bytes 6152 | tf_op jit(solution)/shard_map/ppermute | solution.py:28
  759.7 13.6 %collective-permute-start.49 = (f32[2,1,256]{2,1,0:T(1,128)S(1)}, f32[2,1,256]{2,1,0:T(1,128)S(1)}, u32[]{:S(2)}, u32[]{:S(2)}) collective-permute-start(f32[2,1,256]{2,1,0:T(1,128)S(1)} %get-tuple-element.686), channel_id=1, source_target_pairs={{0,2},{2,4},{4,6},{6,8},{8,10},{10,12},{12,14},{14,16},{16,18},{18... | collective-permute-start | bytes 6152 | tf_op jit(solution)/shard_map/ppermute | solution.py:26
  (33 other events, 192.7 us)
where the time goes:
time: 899 us; the launch traced here: 886 us
  blocking collectives  572 us (64%)
  starting transfers between devices  153 us (17%)
  other arithmetic  52.4 us (6%)
  local copies, waits for them, and re-layouts  48.3 us (5%)
  matrix products  32.9 us (4%)
  between operations  26 us (3%)
    psum x12, blocking collectives, arnoldi(): lax.psum((partial_value, jnp.sum(image * image)), ('sub', 'gx', 'gy'))  499 us
    ppermute x26, starting transfers between devices, padded(): lax.ppermute(tail, axis, [(i, (i + 1) % count) for i in range(ends)])  120 us
    psum x1, blocking collectives, shards(): lax.psum(jnp.sum(forcing * forcing), ('sub', 'gx', 'gy')) + norm_eps  41 us
    another operation x36, other arithmetic  34.7 us
    ppermute x26, starting transfers between devices, padded(): lax.ppermute(head, axis, [((i + 1) % count, i) for i in range(ends)])  33.5 us
    pmax x1, blocking collectives, shards(): column_error = lax.pmax(local_peak, ('sub', 'gx'))  32.4 us
    scatter x23, local copies, waits for them, and re-layouts, arnoldi(): hessenberg.at[:column + 1, column].set(products).at[column + 1, column]  18.1 us
  transfers between devices with their start and end apart: 52, of which 2 were waited for; matrix products, arithmetic and copies ran while one was open for 7% of the time, Pallas kernels for 0%

commit v1 on v0

v1 whole, which is shorter than its diff:
```python
import functools

import jax
import jax.numpy as jnp
from jax import lax
from jax.experimental import pallas as pl
from jax.experimental.pallas import tpu as pltpu
from jax.sharding import PartitionSpec as P

KRYLOV = 12
SUBSTEPS = 4
BLOCK = 4

dt_total = 4.0
sound_sq = 1.0
buoyancy_sq = 0.5
norm_eps = 1e-06
squarings = 4

SIDE = 16
LANES = 128
MESH = pl.DeviceIdType.MESH
HIGH = lax.Precision.HIGHEST


def rise(cells, axis):
    extent = cells.shape[axis]
    return 0.5 * (pltpu.roll(cells, extent - 1, axis) - pltpu.roll(cells, 1, axis))


def wave(vx, vy, b, p):
    return (
        -rise(p, 0),
        -rise(p, 1) + b,
        -buoyancy_sq * vy,
        -sound_sq * (rise(vx, 0) + rise(vy, 1)),
    )


def dot(a, b):
    return jnp.dot(a, b, precision=HIGH, preferred_element_type=jnp.float32)


def kernel(sizes, state, damping, weights, combined, column_error,
           ext, basis, stiff, rows_ref, send, gather, peak_send, peak_gather,
           halo_send, halo_recv, red_send, red_recv, peak_sems):
    n_sub, n_gx, n_gy = sizes
    total = n_sub * n_gx * n_gy
    n_row = n_sub * n_gx
    fields, nx, ny = state.shape
    sub, gx, gy = lax.axis_index("sub"), lax.axis_index("gx"), lax.axis_index("gy")
    row = sub * n_gx + gx
    me = row * n_gy + gy

    def coords(flat):
        line = flat // n_gy
        return (line // n_gx, line % n_gx, flat % n_gy)

    barrier = pltpu.get_barrier_semaphore()

    @pl.loop(1, total)
    def _(d):
        pl.semaphore_signal(barrier, inc=1, device_id=coords((me + d) % total), device_id_type=MESH)

    ext[0, :, 0:nx, 0:ny] = state[...]
    ext[1, :, 0:nx, 0:ny] = damping[...]
    rows_ref[...] = jnp.zeros_like(rows_ref)
    pl.semaphore_wait(barrier, total - 1)

    dirs = [(dr, dc) for dr in (-1, 0, 1) for dc in (-1, 0, 1) if (dr, dc) != (0, 0)]

    def valid(dr, dc):
        r, c = row + dr, gy + dc
        return (r >= 0) & (r < n_row) & (c >= 0) & (c < n_gy)

    def halo_copy(k, a):
        dr, dc = dirs[k]
        r = row + dr
        dev = (r // n_gx, r % n_gx, gy + dc)
        lo = 0 if dc < 0 else ny - LANES
        source = (state, damping)[a]
        src = source if dc == 0 else source.at[:, :, lo : lo + LANES]
        return pltpu.make_async_remote_copy(
            src_ref=src, dst_ref=ext.at[region(a, -dr, -dc)],
            send_sem=halo_send.at[2 * k + a], recv_sem=halo_recv.at[2 * k + a],
            device_id=dev, device_id_type=MESH)

    def region(a, dr, dc):
        r0 = {0: 0, 1: nx, -1: 2 * nx}[dr]
        c0, c1 = {0: (0, ny), 1: (ny, ny + LANES), -1: (ny + LANES, ny + 2 * LANES)}[dc]
        return (a, slice(None), slice(r0, r0 + nx), slice(c0, c1))

    for k, (dr, dc) in enumerate(dirs):
        @pl.when(valid(dr, dc))
        def _(k=k):
            for a in range(2):
                halo_copy(k, a).start()

        @pl.when(jnp.logical_not(valid(dr, dc)))
        def _(dr=dr, dc=dc):
            for a in range(2):
                where = region(a, dr, dc)
                ext[where] = jnp.zeros(ext[where].shape, jnp.float32)

    for k, (dr, dc) in enumerate(dirs):
        @pl.when(valid(-dr, -dc))
        def _(k=k):
            for a in range(2):
                halo_copy(k, a).wait_recv()

        @pl.when(valid(dr, dc))
        def _(k=k):
            for a in range(2):
                halo_copy(k, a).wait_send()

    height, width = 3 * nx, ny + LANES
    lane = lax.broadcasted_iota(jnp.int32, (height, LANES), 1)
    half = lane < LANES // 2

    def extended(a, f):
        side = jnp.where(half, ext[a, f, :, ny : ny + LANES], ext[a, f, :, ny + LANES : ny + 2 * LANES])
        return jnp.concatenate([ext[a, f, :, 0:ny], side], axis=1)

    rr = lax.broadcasted_iota(jnp.int32, (height, width), 0)
    cc = lax.broadcasted_iota(jnp.int32, (height, width), 1)
    has_next, has_prev = (row < n_row - 1).astype(jnp.int32), (row > 0).astype(jnp.int32)
    has_right, has_left = (gy < n_gy - 1).astype(jnp.int32), (gy > 0).astype(jnp.int32)
    row_in = jnp.where(rr < nx, 1, jnp.where(rr < 2 * nx, has_next, has_prev))
    col_in = jnp.where(cc < ny, 1, jnp.where(cc < ny + LANES // 2, has_right, has_left))
    mask = (row_in * col_in).astype(jnp.float32)

    start = [extended(0, f) for f in range(fields)]
    waves = wave(*start)
    for f in range(fields):
        damp = extended(1, f)
        s = start[f]
        stiff[f] = 3.0 * damp * s * s
        basis[0, f] = mask * (waves[f] - damp * s * s * s)

    ri = lax.broadcasted_iota(jnp.int32, (SIDE, SIDE), 0)
    ci = lax.broadcasted_iota(jnp.int32, (SIDE, SIDE), 1)
    eye = ri == ci
    li = lax.broadcasted_iota(jnp.int32, (1, SIDE), 1)

    def to_column(r):
        return jnp.sum(jnp.where(eye, r, 0.0), axis=1, keepdims=True)

    def to_row(c):
        return jnp.sum(jnp.where(eye, c, 0.0), axis=0, keepdims=True)

    def single(x):
        return jnp.sum(jnp.sum(x, axis=1, keepdims=True), axis=0, keepdims=True)

    def combine(columns):
        return jnp.sum(columns, axis=0, keepdims=True)

    gram = jnp.zeros((SIDE, SIDE), jnp.float32)
    hess = jnp.zeros((SIDE, SIDE), jnp.float32)
    beta = None
    syncs = KRYLOV // BLOCK
    for s in range(syncs):
        base = s * BLOCK
        count = base + BLOCK + 1
        if s == 0:
            shift = jnp.full((1, 1), 3.0, jnp.float32)
            back = jnp.full((1, 1), 4.0, jnp.float32)
            grow = jnp.full((1, 1), 5.0, jnp.float32)
        else:
            recent = (ri >= base - 3) & (ri < base)
            third = 1.0 / 3.0
            shift = -third * single(jnp.where(recent & eye, hess, 0.0))
            back = -third * single(jnp.where(recent & (ci == ri - 1), hess, 0.0))
            grow = third * single(jnp.where(recent & (ci == ri + 1), hess, 0.0))
        inverse = 1.0 / grow
        for j in range(BLOCK):
            at = base + j
            current = [basis[at, f] for f in range(fields)]
            waves = wave(*current)
            for f in range(fields):
                image = dt_total * (mask * waves[f] - stiff[f] * current[f]) + shift * current[f]
                if j > 0:
                    image = image + back * basis[at - 1, f]
                basis[at + 1, f] = image * inverse

        first = 0 if s <= 1 else base - BLOCK + 1
        offset, offsets = 0, {}
        for j in range(first, count):
            offsets[j] = offset
            left = basis[j, :, 0:nx, 0:ny]
            for i in range(j + 1):
                prod = left * basis[i, :, 0:nx, 0:ny]
                prod = jnp.sum(prod, axis=0)
                prod = prod.reshape(nx // 8, 8, ny).sum(axis=0)
                acc = prod[:, 0:LANES]
                for t in range(LANES, ny, LANES):
                    acc = acc + prod[:, t : t + LANES]
                rows_ref[offset + i : offset + i + 1, :] = jnp.sum(acc, axis=0, keepdims=True)
            offset += j + 1
        packed = lax.dot_general(
            jnp.ones((8, LANES), jnp.float32), rows_ref[...], (((1,), (1,)), ((), ())),
            precision=HIGH, preferred_element_type=jnp.float32)[0:1, :]
        send[s] = packed
        gather[s, me] = packed

        @pl.loop(1, total)
        def _(d, s=s):
            pltpu.make_async_remote_copy(
                src_ref=send.at[s], dst_ref=gather.at[s, me],
                send_sem=red_send.at[s], recv_sem=red_recv.at[s],
                device_id=coords((me + d) % total), device_id_type=MESH).start()

        everyone = pltpu.make_async_remote_copy(
            src_ref=gather.at[s, pl.ds(0, total - 1)], dst_ref=gather.at[s, pl.ds(0, total - 1)],
            send_sem=red_send.at[s], recv_sem=red_recv.at[s],
            device_id=coords((me + 1) % total), device_id_type=MESH)
        everyone.wait_recv()
        everyone.wait_send()
        summed = jnp.sum(gather[s], axis=0)

        fresh = jnp.zeros((SIDE, LANES), jnp.float32)
        fr = lax.broadcasted_iota(jnp.int32, (SIDE, LANES), 0)
        fl = lax.broadcasted_iota(jnp.int32, (SIDE, LANES), 1)
        for j in range(first, count):
            line = summed if offsets[j] == 0 else pltpu.roll(summed, LANES - offsets[j], 1)
            fresh = jnp.where((fr == j) & (fl <= j), line, fresh)
        lower = fresh[:, 0:SIDE]
        upper = fresh.T[0:SIDE, :]
        old = (ri < first) & (ci < first)
        gram = jnp.where(old, gram, jnp.where(ci <= ri, lower, upper))

        bt = jnp.where(ri < base, hess, 0.0)
        cand = (ri >= base) & (ri < base + BLOCK)
        bt = bt + jnp.where(cand & (ci == ri + 1), grow, 0.0) - jnp.where(cand & eye, shift, 0.0)
        bt = bt - jnp.where(cand & (ri > base) & (ci == ri - 1), back, 0.0)
        btg = dot(bt, gram)

        if s == 0:
            beta = jnp.sqrt(gram[0:1, 0:1] + norm_eps)
            known = ri < 1
            rt = jnp.where(known & eye, 1.0, 0.0) / beta
            grt = jnp.where(known, gram, 0.0) / beta
            r_col = jnp.where(ri[:, 0:1] == 0, 1.0 / beta, 0.0)
        else:
            known = ri <= base
            rt = jnp.where(known & eye, 1.0, 0.0)
            grt = jnp.where(known, gram, 0.0)
            r_col = jnp.where(ri[:, 0:1] == base, 1.0, 0.0)
        for q in range(base, base + BLOCK):
            w = combine(bt * r_col)
            u = combine(btg * r_col)
            h = jnp.sum(rt * u, axis=1, keepdims=True)
            z = w - combine(rt * h)
            gz = u - combine(grt * h)
            squared = jnp.sum(z * gz, axis=1, keepdims=True)
            z_col = to_column(z)
            length = jnp.sqrt(jnp.maximum(squared, 0.0) + norm_eps)
            scale = 1.0 / length
            r_col = z_col * scale
            rt = jnp.where(ri == q + 1, z * scale, rt)
            grt = jnp.where(ri == q + 1, gz * scale, grt)
            hess = jnp.where(ri == q, to_row(h) + jnp.where(li == q + 1, length, 0.0), hess)

        if s < syncs - 1:
            targets = range(0 if s == 0 else base + 1, count)
            coefs = {q: [rt[q : q + 1, j : j + 1] for j in range(count)] for q in targets}

            @pl.loop(0, fields * (height // 8))
            def _(t, targets=targets, coefs=coefs, count=count):
                f, r = t // (height // 8), pl.multiple_of((t % (height // 8)) * 8, 8)
                sums = {q: None for q in targets}
                for j in range(count):
                    vec = basis[j, f, pl.ds(r, 8), :]
                    for q in targets:
                        if j <= q:
                            term = coefs[q][j] * vec
                            sums[q] = term if sums[q] is None else sums[q] + term
                for q in targets:
                    basis[q, f, pl.ds(r, 8), :] = sums[q]

    tail = KRYLOV

    def owned(coef_row):
        out = None
        for j in range(KRYLOV + 1):
            term = coef_row[0:1, j : j + 1].reshape(1, 1, 1) * basis[j, :, 0:nx, 0:ny]
            out = term if out is None else out + term
        return out

    last = owned(rt[tail : tail + 1, :])
    peak = jnp.max(jnp.abs(last), axis=1)
    peak_send[...] = peak
    peak_gather[row] = peak

    @pl.loop(1, n_row)
    def _(d):
        to = (row + d) % n_row
        pltpu.make_async_remote_copy(
            src_ref=peak_send, dst_ref=peak_gather.at[row],
            send_sem=peak_sems.at[0], recv_sem=peak_sems.at[1],
            device_id=(to // n_gx, to % n_gx, gy), device_id_type=MESH).start()

    inside = (ri < KRYLOV) & (ci < KRYLOV)
    x = jnp.where(inside, hess / SUBSTEPS, 0.0) + jnp.where((ri == KRYLOV) & (ci == 0), 1.0, 0.0)
    x = x / 2.0**squarings
    ident = jnp.where(eye, 1.0, 0.0)
    x2 = dot(x, x)
    x3 = dot(x2, x)
    x4 = dot(x2, x2)
    fact = [1.0]
    for d in range(1, 13):
        fact.append(fact[-1] / d)

    def poly(d):
        return fact[d] * ident + fact[d + 1] * x + fact[d + 2] * x2 + fact[d + 3] * x3

    power = poly(0) + dot(x4, poly(4) + dot(x4, poly(8) + fact[12] * x4))
    for repeat in range(squarings):
        power = dot(power, power)
    powers = [None, power]
    for member in range(2, SUBSTEPS + 1):
        powers.append(dot(powers[member // 2], powers[member - member // 2]))
    mixing = jnp.zeros((1, SIDE), jnp.float32)
    highest = jnp.zeros((1, 1), jnp.float32)
    tip = hess[KRYLOV - 1 : KRYLOV, KRYLOV : KRYLOV + 1]
    for member in range(SUBSTEPS):
        line = powers[member + 1][KRYLOV : KRYLOV + 1, :]
        part = (dt_total / SUBSTEPS) * beta * line
        mixing = mixing + weights[member] * part
        fraction = (member + 1) / SUBSTEPS
        highest = jnp.maximum(highest, fraction * tip * jnp.abs(part[:, KRYLOV - 1 : KRYLOV]))
    mixing = jnp.where(li < KRYLOV, mixing, 0.0)
    combined[...] = state[...] + owned(combine(rt * to_column(mixing)))

    around = pltpu.make_async_remote_copy(
        src_ref=peak_gather.at[pl.ds(0, n_row - 1)], dst_ref=peak_gather.at[pl.ds(0, n_row - 1)],
        send_sem=peak_sems.at[0], recv_sem=peak_sems.at[1],
        device_id=coords((me + n_gy) % total), device_id_type=MESH)
    around.wait_recv()
    around.wait_send()
    column_error[...] = highest * jnp.max(peak_gather[...], axis=0)


def shards(sizes, state, damping, weights):
    fields, nx, ny = state.shape
    n_sub, n_gx, n_gy = sizes
    total = n_sub * n_gx * n_gy
    syncs = KRYLOV // BLOCK
    vmem = pl.BlockSpec(memory_space=pltpu.VMEM)
    return pl.pallas_call(
        functools.partial(kernel, sizes),
        out_shape=(
            jax.ShapeDtypeStruct(state.shape, jnp.float32),
            jax.ShapeDtypeStruct((fields, ny), jnp.float32),
        ),
        in_specs=[vmem, vmem, pl.BlockSpec(memory_space=pltpu.SMEM)],
        out_specs=(vmem, vmem),
        scratch_shapes=[
            pltpu.VMEM((2, fields, 3 * nx, ny + 2 * LANES), jnp.float32),
            pltpu.VMEM((KRYLOV + 1, fields, 3 * nx, ny + LANES), jnp.float32),
            pltpu.VMEM((fields, 3 * nx, ny + LANES), jnp.float32),
            pltpu.VMEM((LANES, LANES), jnp.float32),
            pltpu.VMEM((syncs, 1, LANES), jnp.float32),
            pltpu.VMEM((syncs, total, 1, LANES), jnp.float32),
            pltpu.VMEM((fields, ny), jnp.float32),
            pltpu.VMEM((n_sub * n_gx, fields, ny), jnp.float32),
            pltpu.SemaphoreType.DMA((16,)),
            pltpu.SemaphoreType.DMA((16,)),
            pltpu.SemaphoreType.DMA((syncs,)),
            pltpu.SemaphoreType.DMA((syncs,)),
            pltpu.SemaphoreType.DMA((2,)),
        ],
        compiler_params=pltpu.CompilerParams(
            collective_id=0, has_side_effects=True, vmem_limit_bytes=48 * 2**20),
    )(state, damping, weights)


def solution(mesh):
    sizes = (mesh.shape["sub"], mesh.shape["gx"], mesh.shape["gy"])
    return jax.shard_map(
        functools.partial(shards, sizes),
        mesh=mesh,
        in_specs=(P(None, ("sub", "gx"), "gy"), P(None, ("sub", "gx"), "gy"), P()),
        out_specs=(P(None, ("sub", "gx"), "gy"), P(None, "gy")),
        check_vma=False,
    )
```

time: 899 us -> 55 us (0.06); the launches traced: 886 us -> 54.8 us
  blocking collectives: 572 us -> 0 us
  starting transfers between devices: 153 us -> 0 us
  other arithmetic: 52.4 us -> 0 us
  Pallas kernels: 0 us -> 50.6 us
  local copies, waits for them, and re-layouts: 48.3 us -> 3.55 us
  matrix products: 32.9 us -> 0 us
  between operations: 26 us -> 0.65 us
    psum x13 -> x0, blocking collectives: 540 us -> none  [the longest x12 499 us: arnoldi(): lax.psum((partial_value, jnp.sum(image * image)), ('sub', 'gx', 'gy'))]
    ppermute x52 -> x0, starting transfers between devices: 153 us -> none  [the longest x26 120 us: padded(): lax.ppermute(tail, axis, [(i, (i + 1) % count) for i in range(ends)])]
    pallas_call x0 -> x1, Pallas kernels: none -> 50.6 us  [shards(): pl.pallas_call(functools.partial(kernel, sizes), out_shape=(jax.ShapeDtyp...]
    another operation x38 -> x0, other arithmetic: 34.8 us -> none
    dot_general x103 -> x0, matrix products: 32.9 us -> none  [the longest x11 14 us: arnoldi(): jnp.dot(basis[:column + 1], image, precision=lax.Precision.HIGHEST)]
    pmax x1 -> x0, blocking collectives: 32.4 us -> none  [shards(): column_error = lax.pmax(local_peak, ('sub', 'gx'))]
    scatter x43 -> x0, local copies, waits for them, and re-layouts: 31.5 us -> none  [the longest x23 18.1 us: arnoldi(): hessenberg.at[:column + 1, column].set(products).at[column + 1, column]]
    reduce_sum x23 -> x0, other arithmetic: 14.1 us -> none  [the longest x11 6.86 us: arnoldi(): jnp.sum(image * image)]
  transfers between devices with their start and end apart: 52 -> 0, of which waited for: 2 -> 0; matrix products, arithmetic and copies ran while one was open for 7% -> 0% of each run, Pallas kernels for 0% -> 0%
where the time goes in v1:
time: 55 us; the launch traced here: 54.8 us
  Pallas kernels  50.6 us (92%)
  local copies, waits for them, and re-layouts  3.55 us (6%)
  between operations  0.65 us (1%)
    pallas_call x1, Pallas kernels, shards(): pl.pallas_call(functools.partial(kernel, sizes), out_shape=(jax.ShapeDtyp...  50.6 us
    unnamed x8, local copies, waits for them, and re-layouts  3.55 us

profile of v1, /device:TPU:0, one launch (start us, length us, event | category | flops | bytes accessed | tf_op | source)
XLA Modules:
  0.0 54.8 jit_solution(9629991581753671144)
XLA Ops:
  0.6 0.0 copy-start
  0.6 0.8 %copy-done = f32[4,16,256]{2,1,0:T(8,128)S(1)} copy-done((f32[4,16,256]{2,1,0:T(8,128)S(1)}, f32[4,16,256]{2,1,0:T(8,128)}, u32[]{:S(2)}) %copy-start) | copy-done | bytes 65560
  1.5 0.0 copy-start.1
  1.5 0.8 %copy-done.1 = f32[4,16,256]{2,1,0:T(8,128)S(1)} copy-done((f32[4,16,256]{2,1,0:T(8,128)S(1)}, f32[4,16,256]{2,1,0:T(8,128)}, u32[]{:S(2)}) %copy-start.1) | copy-done | bytes 65560
  2.3 0.0 copy-start.2
  2.3 0.7 %copy-done.2 = f32[4]{0:T(128)S(1)} copy-done((f32[4]{0:T(128)S(1)}, f32[4]{0:T(128)}, u32[]{:S(2)}) %copy-start.2) | copy-done | bytes 40
  3.0 50.6 %shard_map.50 = (f32[4,16,256]{2,1,0:T(8,128)S(1)}, f32[4,256]{1,0:T(4,128)S(1)}) custom-call(f32[4,16,256]{2,1,0:T(8,128)S(1)} %copy-done, f32[4,16,256]{2,1,0:T(8,128)S(1)} %copy-done.1, f32[4]{0:T(128)S(1)} %copy-done.2), custom_call_target="tpu_custom_call" | custom-call | tf_op jit(solution)/shard_map/pallas_call | solution.py:349
  53.6 0.6 %copy.7 = f32[4,16,256]{2,1,0:T(8,128)} copy(f32[4,16,256]{2,1,0:T(8,128)S(1)} %get-tuple-element.4) | data formatting | bytes 131072
  54.2 0.6 %copy.8 = f32[4,256]{1,0:T(4,128)} copy(f32[4,256]{1,0:T(4,128)S(1)} %get-tuple-element.5) | data formatting | bytes 8192
Async XLA Ops:
  0.6 0.8 %copy-start = (f32[4,16,256]{2,1,0:T(8,128)S(1)}, f32[4,16,256]{2,1,0:T(8,128)}, u32[]{:S(2)}) copy-start(f32[4,16,256]{2,1,0:T(8,128)} %state.1) | copy-start | bytes 196612
  1.5 0.8 %copy-start.1 = (f32[4,16,256]{2,1,0:T(8,128)S(1)}, f32[4,16,256]{2,1,0:T(8,128)}, u32[]{:S(2)}) copy-start(f32[4,16,256]{2,1,0:T(8,128)} %damping.1) | copy-start | bytes 196612
  2.3 0.7 %copy-start.2 = (f32[4]{0:T(128)S(1)}, f32[4]{0:T(128)}, u32[]{:S(2)}) copy-start(f32[4]{0:T(128)} %weights.1) | copy-start | bytes 52

commit v2 on v1

--- a/solution.py
+++ b/solution.py
@@ -42,8 +42,8 @@
 
 
 def kernel(sizes, state, damping, weights, combined, column_error,
-           ext, basis, stiff, rows_ref, send, gather, peak_send, peak_gather,
-           halo_send, halo_recv, red_send, red_recv, peak_sems):
+           ext, edge_send, edge_recv, basis, begin, stiff, rows_ref, send, gather,
+           peak_send, peak_gather, load_sems, halo_send, halo_recv, red_send, red_recv, peak_sems):
     n_sub, n_gx, n_gy = sizes
     total = n_sub * n_gx * n_gy
     n_row = n_sub * n_gx
@@ -57,69 +57,124 @@
         return (line // n_gx, line % n_gx, flat % n_gy)
 
     barrier = pltpu.get_barrier_semaphore()
-
-    @pl.loop(1, total)
-    def _(d):
-        pl.semaphore_signal(barrier, inc=1, device_id=coords((me + d) % total), device_id_type=MESH)
-
-    ext[0, :, 0:nx, 0:ny] = state[...]
-    ext[1, :, 0:nx, 0:ny] = damping[...]
+    loads = [
+        pltpu.make_async_copy(src, ext.at[a, :, 0:nx, :], load_sems.at[a])
+        for a, src in enumerate((state, damping))
+    ]
+    for load in loads:
+        load.start()
+
+    subs = [lax.rem(sub + d, n_sub) for d in range(n_sub)]
+    gxs = [lax.rem(gx + d, n_gx) for d in range(n_gx)]
+    gys = [lax.rem(gy + d, n_gy) for d in range(n_gy)]
+
+    def ring(d, extent):
+        return min(d, extent - d)
+
+    others = sorted(
+        ((a, b, c) for a in range(n_sub) for b in range(n_gx) for c in range(n_gy)),
+        key=lambda o: -(ring(o[1], n_gx) + ring(o[0], n_sub) + ring(o[2], n_gy)))[:-1]
+
+    def each_other(visit):
+        if total <= 64:
+            for a, b, c in others:
+                visit((subs[a], gxs[b], gys[c]))
+        else:
+            @pl.loop(1, total)
+            def _(d):
+                visit(coords((me + d) % total))
+
+    each_other(lambda dev: pl.semaphore_signal(barrier, inc=1, device_id=dev, device_id_type=MESH))
+
     rows_ref[...] = jnp.zeros_like(rows_ref)
+    begin[...] = jnp.zeros_like(begin)
+    for load in loads:
+        load.wait()
+
+    edge = LANES // (2 * fields)
+    tile_lane = lax.broadcasted_iota(jnp.int32, (nx, LANES), 1)
+    for side in range(2):
+        packed = jnp.zeros((nx, LANES), jnp.float32)
+        for a in range(2):
+            for f in range(fields):
+                g = a * fields + f
+                lo = 0 if side == 0 else ny - LANES
+                turn = (edge * g + (0 if side == 0 else edge)) % LANES
+                tile = ext[a, f, 0:nx, lo : lo + LANES]
+                tile = tile if turn == 0 else pltpu.roll(tile, turn, 1)
+                packed = jnp.where(tile_lane // edge == g, tile, packed)
+        edge_send[side] = packed
     pl.semaphore_wait(barrier, total - 1)
 
-    dirs = [(dr, dc) for dr in (-1, 0, 1) for dc in (-1, 0, 1) if (dr, dc) != (0, 0)]
+    dirs = [(dr, dc) for dr in (-1, 1) for dc in (0, -1, 1)] + [(0, -1), (0, 1)]
+    offset_of = {0: 0, 1: nx, -1: 2 * nx}
 
     def valid(dr, dc):
         r, c = row + dr, gy + dc
         return (r >= 0) & (r < n_row) & (c >= 0) & (c < n_gy)
 
-    def halo_copy(k, a):
+    def landing(dr, dc):
+        return edge_recv.at[dr + 1, (dc + 1) // 2]
+
+    def halo_copies(k):
         dr, dc = dirs[k]
         r = row + dr
         dev = (r // n_gx, r % n_gx, gy + dc)
-        lo = 0 if dc < 0 else ny - LANES
-        source = (state, damping)[a]
-        src = source if dc == 0 else source.at[:, :, lo : lo + LANES]
-        return pltpu.make_async_remote_copy(
-            src_ref=src, dst_ref=ext.at[region(a, -dr, -dc)],
-            send_sem=halo_send.at[2 * k + a], recv_sem=halo_recv.at[2 * k + a],
-            device_id=dev, device_id_type=MESH)
-
-    def region(a, dr, dc):
-        r0 = {0: 0, 1: nx, -1: 2 * nx}[dr]
-        c0, c1 = {0: (0, ny), 1: (ny, ny + LANES), -1: (ny + LANES, ny + 2 * LANES)}[dc]
-        return (a, slice(None), slice(r0, r0 + nx), slice(c0, c1))
+        if dc == 0:
+            o = offset_of[-dr]
+            pairs = [(ext.at[a, :, 0:nx, :], ext.at[a, :, o : o + nx, :]) for a in range(2)]
+        else:
+            pairs = [(edge_send.at[(dc + 1) // 2], landing(-dr, -dc))]
+        return [
+            pltpu.make_async_remote_copy(
+                src_ref=src, dst_ref=dst,
+                send_sem=halo_send.at[2 * k + n], recv_sem=halo_recv.at[2 * k + n],
+                device_id=dev, device_id_type=MESH)
+            for n, (src, dst) in enumerate(pairs)
+        ]
 
     for k, (dr, dc) in enumerate(dirs):
         @pl.when(valid(dr, dc))
         def _(k=k):
-            for a in range(2):
-                halo_copy(k, a).start()
+            for copy in halo_copies(k):
+                copy.start()
 
         @pl.when(jnp.logical_not(valid(dr, dc)))
         def _(dr=dr, dc=dc):
-            for a in range(2):
-                where = region(a, dr, dc)
-                ext[where] = jnp.zeros(ext[where].shape, jnp.float32)
+            if dc == 0:
+                o = offset_of[dr]
+                ext[:, :, o : o + nx, :] = jnp.zeros((2, fields, nx, ny), jnp.float32)
+            else:
+                edge_recv[dr + 1, (dc + 1) // 2] = jnp.zeros((nx, LANES), jnp.float32)
 
     for k, (dr, dc) in enumerate(dirs):
         @pl.when(valid(-dr, -dc))
         def _(k=k):
-            for a in range(2):
-                halo_copy(k, a).wait_recv()
+            for copy in halo_copies(k):
+                copy.wait_recv()
 
         @pl.when(valid(dr, dc))
         def _(k=k):
-            for a in range(2):
-                halo_copy(k, a).wait_send()
+            for copy in halo_copies(k):
+                copy.wait_send()
 
     height, width = 3 * nx, ny + LANES
     lane = lax.broadcasted_iota(jnp.int32, (height, LANES), 1)
-    half = lane < LANES // 2
+    sides = [
+        jnp.concatenate([edge_recv[1, side], edge_recv[2, side], edge_recv[0, side]], axis=0)
+        for side in range(2)
+    ]
 
     def extended(a, f):
-        side = jnp.where(half, ext[a, f, :, ny : ny + LANES], ext[a, f, :, ny + LANES : ny + 2 * LANES])
-        return jnp.concatenate([ext[a, f, :, 0:ny], side], axis=1)
+        g = a * fields + f
+
+        def turned(cells, by):
+            return cells if by % LANES == 0 else pltpu.roll(cells, by % LANES, 1)
+
+        left = turned(sides[0], -edge * g - edge)
+        right = turned(sides[1], -edge * g)
+        side = jnp.where(lane < edge, right, jnp.where(lane >= LANES - edge, left, 0.0))
+        return jnp.concatenate([ext[a, f], side], axis=1)
 
     rr = lax.broadcasted_iota(jnp.int32, (height, width), 0)
     cc = lax.broadcasted_iota(jnp.int32, (height, width), 1)
@@ -154,7 +209,8 @@
     def combine(columns):
         return jnp.sum(columns, axis=0, keepdims=True)
 
-    gram = jnp.zeros((SIDE, SIDE), jnp.float32)
+    raw_gram = jnp.zeros((SIDE, SIDE), jnp.float32)
+    raw_rt = jnp.zeros((SIDE, SIDE), jnp.float32)
     hess = jnp.zeros((SIDE, SIDE), jnp.float32)
     beta = None
     syncs = KRYLOV // BLOCK
@@ -174,15 +230,17 @@
         inverse = 1.0 / grow
         for j in range(BLOCK):
             at = base + j
-            current = [basis[at, f] for f in range(fields)]
+            source = begin if j == 0 and s > 0 else basis.at[at]
+            before = begin if j == 1 and s > 0 else basis.at[max(at - 1, 0)]
+            current = [source[f] for f in range(fields)]
             waves = wave(*current)
             for f in range(fields):
                 image = dt_total * (mask * waves[f] - stiff[f] * current[f]) + shift * current[f]
                 if j > 0:
-                    image = image + back * basis[at - 1, f]
+                    image = image + back * before[f]
                 basis[at + 1, f] = image * inverse
 
-        first = 0 if s <= 1 else base - BLOCK + 1
+        first = 0 if s == 0 else base + 1
         offset, offsets = 0, {}
         for j in range(first, count):
             offsets[j] = offset
@@ -202,12 +260,10 @@
         send[s] = packed
         gather[s, me] = packed
 
-        @pl.loop(1, total)
-        def _(d, s=s):
-            pltpu.make_async_remote_copy(
-                src_ref=send.at[s], dst_ref=gather.at[s, me],
-                send_sem=red_send.at[s], recv_sem=red_recv.at[s],
-                device_id=coords((me + d) % total), device_id_type=MESH).start()
+        each_other(lambda dev, s=s: pltpu.make_async_remote_copy(
+            src_ref=send.at[s], dst_ref=gather.at[s, me],
+            send_sem=red_send.at[s], recv_sem=red_recv.at[s],
+            device_id=dev, device_id_type=MESH).start())
 
         everyone = pltpu.make_async_remote_copy(
             src_ref=gather.at[s, pl.ds(0, total - 1)], dst_ref=gather.at[s, pl.ds(0, total - 1)],
@@ -226,7 +282,14 @@
         lower = fresh[:, 0:SIDE]
         upper = fresh.T[0:SIDE, :]
         old = (ri < first) & (ci < first)
-        gram = jnp.where(old, gram, jnp.where(ci <= ri, lower, upper))
+        raw_gram = jnp.where(old, raw_gram, jnp.where(ci <= ri, lower, upper))
+        if s == 0:
+            gram = raw_gram
+        else:
+            frame = jnp.where(ri <= base, raw_rt, jnp.where(eye, 1.0, 0.0))
+            gram = lax.dot_general(
+                dot(frame, raw_gram), frame, (((1,), (1,)), ((), ())),
+                precision=HIGH, preferred_element_type=jnp.float32)
 
         bt = jnp.where(ri < base, hess, 0.0)
         cand = (ri >= base) & (ri < base + BLOCK)
@@ -260,22 +323,18 @@
             grt = jnp.where(ri == q + 1, gz * scale, grt)
             hess = jnp.where(ri == q, to_row(h) + jnp.where(li == q + 1, length, 0.0), hess)
 
+        raw_rt = rt if s == 0 else dot(rt, frame)
         if s < syncs - 1:
-            targets = range(0 if s == 0 else base + 1, count)
-            coefs = {q: [rt[q : q + 1, j : j + 1] for j in range(count)] for q in targets}
-
-            @pl.loop(0, fields * (height // 8))
-            def _(t, targets=targets, coefs=coefs, count=count):
-                f, r = t // (height // 8), pl.multiple_of((t % (height // 8)) * 8, 8)
-                sums = {q: None for q in targets}
-                for j in range(count):
-                    vec = basis[j, f, pl.ds(r, 8), :]
-                    for q in targets:
-                        if j <= q:
-                            term = coefs[q][j] * vec
-                            sums[q] = term if sums[q] is None else sums[q] + term
-                for q in targets:
-                    basis[q, f, pl.ds(r, 8), :] = sums[q]
+            top = count - 1
+            coefs = [raw_rt[top : top + 1, j : j + 1] for j in range(count)]
+            tiles = list(range((nx + 8) // 8)) + [height // 8 - 1]
+            for f in range(fields):
+                for t in tiles:
+                    out = None
+                    for j in range(count):
+                        term = coefs[j] * basis[j, f, 8 * t : 8 * t + 8, :]
+                        out = term if out is None else out + term
+                    begin[f, 8 * t : 8 * t + 8, :] = out
 
     tail = KRYLOV
 
@@ -286,7 +345,7 @@
             out = term if out is None else out + term
         return out
 
-    last = owned(rt[tail : tail + 1, :])
+    last = owned(raw_rt[tail : tail + 1, :])
     peak = jnp.max(jnp.abs(last), axis=1)
     peak_send[...] = peak
     peak_gather[row] = peak
@@ -329,7 +388,7 @@
         fraction = (member + 1) / SUBSTEPS
         highest = jnp.maximum(highest, fraction * tip * jnp.abs(part[:, KRYLOV - 1 : KRYLOV]))
     mixing = jnp.where(li < KRYLOV, mixing, 0.0)
-    combined[...] = state[...] + owned(combine(rt * to_column(mixing)))
+    combined[...] = ext[0, :, 0:nx, :] + owned(combine(raw_rt * to_column(mixing)))
 
     around = pltpu.make_async_remote_copy(
         src_ref=peak_gather.at[pl.ds(0, n_row - 1)], dst_ref=peak_gather.at[pl.ds(0, n_row - 1)],
@@ -352,17 +411,21 @@
             jax.ShapeDtypeStruct(state.shape, jnp.float32),
             jax.ShapeDtypeStruct((fields, ny), jnp.float32),
         ),
-        in_specs=[vmem, vmem, pl.BlockSpec(memory_space=pltpu.SMEM)],
+        in_specs=[pl.BlockSpec(memory_space=pl.ANY)] * 2 + [pl.BlockSpec(memory_space=pltpu.SMEM)],
         out_specs=(vmem, vmem),
         scratch_shapes=[
-            pltpu.VMEM((2, fields, 3 * nx, ny + 2 * LANES), jnp.float32),
+            pltpu.VMEM((2, fields, 3 * nx, ny), jnp.float32),
+            pltpu.VMEM((2, nx, LANES), jnp.float32),
+            pltpu.VMEM((3, 2, nx, LANES), jnp.float32),
             pltpu.VMEM((KRYLOV + 1, fields, 3 * nx, ny + LANES), jnp.float32),
+            pltpu.VMEM((fields, 3 * nx, ny + LANES), jnp.float32),
             pltpu.VMEM((fields, 3 * nx, ny + LANES), jnp.float32),
             pltpu.VMEM((LANES, LANES), jnp.float32),
             pltpu.VMEM((syncs, 1, LANES), jnp.float32),
             pltpu.VMEM((syncs, total, 1, LANES), jnp.float32),
             pltpu.VMEM((fields, ny), jnp.float32),
             pltpu.VMEM((n_sub * n_gx, fields, ny), jnp.float32),
+            pltpu.SemaphoreType.DMA((2,)),
             pltpu.SemaphoreType.DMA((16,)),
             pltpu.SemaphoreType.DMA((16,)),
             pltpu.SemaphoreType.DMA((syncs,)),

time: 55 us -> 45.3 us (0.82)
  Pallas kernels: 50.6 us -> 40.9 us
    pallas_call x1, Pallas kernels: 50.6 us -> 40.9 us  [shards(): pl.pallas_call(functools.partial(kernel, sizes), out_shape=(jax.ShapeDtyp...]
where the time goes in v2:
time: 45.3 us; the launch traced here: 45.1 us
  Pallas kernels  40.9 us (90%)
  local copies, waits for them, and re-layouts  3.55 us (8%)
  between operations  0.65 us (1%)
    pallas_call x1, Pallas kernels, shards(): pl.pallas_call(functools.partial(kernel, sizes), out_shape=(jax.ShapeDtyp...  40.9 us
    unnamed x8, local copies, waits for them, and re-layouts  3.55 us

profile of v2, /device:TPU:0, one launch (start us, length us, event | category | flops | bytes accessed | tf_op | source)
XLA Modules:
  0.0 45.1 jit_solution(8138980502740799265)
XLA Ops:
  0.6 0.0 copy-start
  0.6 0.8 %copy-done = f32[4,16,256]{2,1,0:T(8,128)S(1)} copy-done((f32[4,16,256]{2,1,0:T(8,128)S(1)}, f32[4,16,256]{2,1,0:T(8,128)}, u32[]{:S(2)}) %copy-start) | copy-done | bytes 65560
  1.5 0.0 copy-start.1
  1.5 0.8 %copy-done.1 = f32[4,16,256]{2,1,0:T(8,128)S(1)} copy-done((f32[4,16,256]{2,1,0:T(8,128)S(1)}, f32[4,16,256]{2,1,0:T(8,128)}, u32[]{:S(2)}) %copy-start.1) | copy-done | bytes 65560
  2.3 0.0 copy-start.2
  2.3 0.7 %copy-done.2 = f32[4]{0:T(128)S(1)} copy-done((f32[4]{0:T(128)S(1)}, f32[4]{0:T(128)}, u32[]{:S(2)}) %copy-start.2) | copy-done | bytes 40
  3.0 40.9 %shard_map.50 = (f32[4,16,256]{2,1,0:T(8,128)S(1)}, f32[4,256]{1,0:T(4,128)S(1)}) custom-call(f32[4,16,256]{2,1,0:T(8,128)S(1)} %copy-done, f32[4,16,256]{2,1,0:T(8,128)S(1)} %copy-done.1, f32[4]{0:T(128)S(1)} %copy-done.2), custom_call_target="tpu_custom_call" | custom-call | tf_op jit(solution)/shard_map/pallas_call | solution.py:408
  43.9 0.6 %copy.7 = f32[4,16,256]{2,1,0:T(8,128)} copy(f32[4,16,256]{2,1,0:T(8,128)S(1)} %get-tuple-element.4) | data formatting | bytes 131072
  44.5 0.6 %copy.8 = f32[4,256]{1,0:T(4,128)} copy(f32[4,256]{1,0:T(4,128)S(1)} %get-tuple-element.5) | data formatting | bytes 8192
Async XLA Ops:
  0.6 0.8 %copy-start = (f32[4,16,256]{2,1,0:T(8,128)S(1)}, f32[4,16,256]{2,1,0:T(8,128)}, u32[]{:S(2)}) copy-start(f32[4,16,256]{2,1,0:T(8,128)} %state.1) | copy-start | bytes 196612
  1.5 0.8 %copy-start.1 = (f32[4,16,256]{2,1,0:T(8,128)S(1)}, f32[4,16,256]{2,1,0:T(8,128)}, u32[]{:S(2)}) copy-start(f32[4,16,256]{2,1,0:T(8,128)} %damping.1) | copy-start | bytes 196612
  2.3 0.7 %copy-start.2 = (f32[4]{0:T(128)S(1)}, f32[4]{0:T(128)}, u32[]{:S(2)}) copy-start(f32[4]{0:T(128)} %weights.1) | copy-start | bytes 52

commit v3 on v2

--- a/solution.py
+++ b/solution.py
@@ -41,8 +41,8 @@
     return jnp.dot(a, b, precision=HIGH, preferred_element_type=jnp.float32)
 
 
-def kernel(sizes, state, damping, weights, combined, column_error,
-           ext, edge_send, edge_recv, basis, begin, stiff, rows_ref, send, gather,
+def kernel(sizes, state, damping, weights_in, combined, column_error,
+           weights, ext, edge_send, edge_recv, near_basis, near_stiff, basis, begin, stiff, rows_ref, send, gather,
            peak_send, peak_gather, load_sems, halo_send, halo_recv, red_send, red_recv, peak_sems):
     n_sub, n_gx, n_gy = sizes
     total = n_sub * n_gx * n_gy
@@ -61,6 +61,7 @@
         pltpu.make_async_copy(src, ext.at[a, :, 0:nx, :], load_sems.at[a])
         for a, src in enumerate((state, damping))
     ]
+    loads.append(pltpu.make_async_copy(weights_in, weights, load_sems.at[2]))
     for load in loads:
         load.start()
 
@@ -116,19 +117,21 @@
     def landing(dr, dc):
         return edge_recv.at[dr + 1, (dc + 1) // 2]
 
-    def halo_copies(k):
+    def halo_copies(k, deep):
         dr, dc = dirs[k]
         r = row + dr
         dev = (r // n_gx, r % n_gx, gy + dc)
         if dc == 0:
             o = offset_of[-dr]
-            pairs = [(ext.at[a, :, 0:nx, :], ext.at[a, :, o : o + nx, :]) for a in range(2)]
+            cut = nx - 8 if dr > 0 else 8
+            lo, hi = (cut, nx) if (dr > 0) != deep else (0, cut)
+            pairs = [(ext.at[a, :, lo:hi, :], ext.at[a, :, o + lo : o + hi, :]) for a in range(2)]
         else:
             pairs = [(edge_send.at[(dc + 1) // 2], landing(-dr, -dc))]
         return [
             pltpu.make_async_remote_copy(
                 src_ref=src, dst_ref=dst,
-                send_sem=halo_send.at[2 * k + n], recv_sem=halo_recv.at[2 * k + n],
+                send_sem=halo_send.at[4 * k + 2 * deep + n], recv_sem=halo_recv.at[4 * k + 2 * deep + n],
                 device_id=dev, device_id_type=MESH)
             for n, (src, dst) in enumerate(pairs)
         ]
@@ -136,7 +139,7 @@
     for k, (dr, dc) in enumerate(dirs):
         @pl.when(valid(dr, dc))
         def _(k=k):
-            for copy in halo_copies(k):
+            for copy in halo_copies(k, False):
                 copy.start()
 
         @pl.when(jnp.logical_not(valid(dr, dc)))
@@ -148,15 +151,21 @@
                 edge_recv[dr + 1, (dc + 1) // 2] = jnp.zeros((nx, LANES), jnp.float32)
 
     for k, (dr, dc) in enumerate(dirs):
-        @pl.when(valid(-dr, -dc))
-        def _(k=k):
-            for copy in halo_copies(k):
-                copy.wait_recv()
-
-        @pl.when(valid(dr, dc))
-        def _(k=k):
-            for copy in halo_copies(k):
-                copy.wait_send()
+        if dc == 0:
+            @pl.when(valid(dr, dc))
+            def _(k=k):
+                for copy in halo_copies(k, True):
+                    copy.start()
+
+    def arrive(deep):
+        for k, (dr, dc) in enumerate(dirs):
+            if dc == 0 or not deep:
+                @pl.when(valid(-dr, -dc))
+                def _(k=k):
+                    for copy in halo_copies(k, deep):
+                        copy.wait_recv()
+
+    arrive(False)
 
     height, width = 3 * nx, ny + LANES
     lane = lax.broadcasted_iota(jnp.int32, (height, LANES), 1)
@@ -165,16 +174,26 @@
         for side in range(2)
     ]
 
-    def extended(a, f):
+    def close(cells):
+        return jnp.concatenate([cells[0 : nx + 8], cells[height - 8 : height]], axis=0)
+
+    def extended(a, f, near):
         g = a * fields + f
+        pick = close if near else lambda cells: cells
 
         def turned(cells, by):
+            cells = pick(cells)
             return cells if by % LANES == 0 else pltpu.roll(cells, by % LANES, 1)
 
         left = turned(sides[0], -edge * g - edge)
         right = turned(sides[1], -edge * g)
-        side = jnp.where(lane < edge, right, jnp.where(lane >= LANES - edge, left, 0.0))
-        return jnp.concatenate([ext[a, f], side], axis=1)
+        at = pick(lane)
+        side = jnp.where(at < edge, right, jnp.where(at >= LANES - edge, left, 0.0))
+        if near:
+            cells = jnp.concatenate([ext[a, f, 0 : nx + 8], ext[a, f, height - 8 : height]], axis=0)
+        else:
+            cells = ext[a, f]
+        return jnp.concatenate([cells, side], axis=1)
 
     rr = lax.broadcasted_iota(jnp.int32, (height, width), 0)
     cc = lax.broadcasted_iota(jnp.int32, (height, width), 1)
@@ -184,13 +203,16 @@
     col_in = jnp.where(cc < ny, 1, jnp.where(cc < ny + LANES // 2, has_right, has_left))
     mask = (row_in * col_in).astype(jnp.float32)
 
-    start = [extended(0, f) for f in range(fields)]
-    waves = wave(*start)
-    for f in range(fields):
-        damp = extended(1, f)
-        s = start[f]
-        stiff[f] = 3.0 * damp * s * s
-        basis[0, f] = mask * (waves[f] - damp * s * s * s)
+    def initial(near):
+        into, rates = (near_basis, near_stiff) if near else (basis, stiff)
+        valid_cells = close(mask) if near else mask
+        start = [extended(0, f, near) for f in range(fields)]
+        waves = wave(*start)
+        for f in range(fields):
+            damp = extended(1, f, near)
+            s = start[f]
+            rates[f] = 3.0 * damp * s * s
+            into[0, f] = valid_cells * (waves[f] - damp * s * s * s)
 
     ri = lax.broadcasted_iota(jnp.int32, (SIDE, SIDE), 0)
     ci = lax.broadcasted_iota(jnp.int32, (SIDE, SIDE), 1)
@@ -213,6 +235,7 @@
     raw_rt = jnp.zeros((SIDE, SIDE), jnp.float32)
     hess = jnp.zeros((SIDE, SIDE), jnp.float32)
     beta = None
+    sent = []
     syncs = KRYLOV // BLOCK
     for s in range(syncs):
         base = s * BLOCK
@@ -228,25 +251,35 @@
             back = -third * single(jnp.where(recent & (ci == ri - 1), hess, 0.0))
             grow = third * single(jnp.where(recent & (ci == ri + 1), hess, 0.0))
         inverse = 1.0 / grow
-        for j in range(BLOCK):
-            at = base + j
-            source = begin if j == 0 and s > 0 else basis.at[at]
-            before = begin if j == 1 and s > 0 else basis.at[max(at - 1, 0)]
-            current = [source[f] for f in range(fields)]
-            waves = wave(*current)
-            for f in range(fields):
-                image = dt_total * (mask * waves[f] - stiff[f] * current[f]) + shift * current[f]
-                if j > 0:
-                    image = image + back * before[f]
-                basis[at + 1, f] = image * inverse
+
+        def candidates(near, s=s, base=base, shift=shift, back=back, inverse=inverse):
+            into, rates = (near_basis, near_stiff) if near else (basis, stiff)
+            valid_cells = close(mask) if near else mask
+            for j in range(BLOCK):
+                at = base + j
+                source = begin if j == 0 and s > 0 else into.at[at]
+                before = begin if j == 1 and s > 0 else into.at[max(at - 1, 0)]
+                current = [source[f] for f in range(fields)]
+                waves = wave(*current)
+                for f in range(fields):
+                    image = dt_total * (valid_cells * waves[f] - rates[f] * current[f])
+                    image = image + shift * current[f]
+                    if j > 0:
+                        image = image + back * before[f]
+                    into[at + 1, f] = image * inverse
+
+        if s == 0:
+            initial(True)
+        candidates(s == 0)
+        vectors = near_basis if s == 0 else basis
 
         first = 0 if s == 0 else base + 1
         offset, offsets = 0, {}
         for j in range(first, count):
             offsets[j] = offset
-            left = basis[j, :, 0:nx, 0:ny]
+            left = vectors[j, :, 0:nx, 0:ny]
             for i in range(j + 1):
-                prod = left * basis[i, :, 0:nx, 0:ny]
+                prod = left * vectors[i, :, 0:nx, 0:ny]
                 prod = jnp.sum(prod, axis=0)
                 prod = prod.reshape(nx // 8, 8, ny).sum(axis=0)
                 acc = prod[:, 0:LANES]
@@ -265,12 +298,16 @@
             send_sem=red_send.at[s], recv_sem=red_recv.at[s],
             device_id=dev, device_id_type=MESH).start())
 
+        if s == 0:
+            arrive(True)
+            initial(False)
+            candidates(False)
         everyone = pltpu.make_async_remote_copy(
             src_ref=gather.at[s, pl.ds(0, total - 1)], dst_ref=gather.at[s, pl.ds(0, total - 1)],
             send_sem=red_send.at[s], recv_sem=red_recv.at[s],
             device_id=coords((me + 1) % total), device_id_type=MESH)
         everyone.wait_recv()
-        everyone.wait_send()
+        sent.append(everyone)
         summed = jnp.sum(gather[s], axis=0)
 
         fresh = jnp.zeros((SIDE, LANES), jnp.float32)
@@ -395,7 +432,14 @@
         send_sem=peak_sems.at[0], recv_sem=peak_sems.at[1],
         device_id=coords((me + n_gy) % total), device_id_type=MESH)
     around.wait_recv()
-    around.wait_send()
+    for copy in sent + [around]:
+        copy.wait_send()
+    for k, (dr, dc) in enumerate(dirs):
+        @pl.when(valid(dr, dc))
+        def _(k=k, dc=dc):
+            for copy in halo_copies(k, False) + (halo_copies(k, True) if dc == 0 else []):
+                copy.wait_send()
+
     column_error[...] = highest * jnp.max(peak_gather[...], axis=0)
 
 
@@ -411,12 +455,15 @@
             jax.ShapeDtypeStruct(state.shape, jnp.float32),
             jax.ShapeDtypeStruct((fields, ny), jnp.float32),
         ),
-        in_specs=[pl.BlockSpec(memory_space=pl.ANY)] * 2 + [pl.BlockSpec(memory_space=pltpu.SMEM)],
+        in_specs=[pl.BlockSpec(memory_space=pltpu.HBM)] * 3,
         out_specs=(vmem, vmem),
         scratch_shapes=[
+            pltpu.SMEM(weights.shape, jnp.float32),
             pltpu.VMEM((2, fields, 3 * nx, ny), jnp.float32),
             pltpu.VMEM((2, nx, LANES), jnp.float32),
             pltpu.VMEM((3, 2, nx, LANES), jnp.float32),
+            pltpu.VMEM((BLOCK + 1, fields, nx + 16, ny + LANES), jnp.float32),
+            pltpu.VMEM((fields, nx + 16, ny + LANES), jnp.float32),
             pltpu.VMEM((KRYLOV + 1, fields, 3 * nx, ny + LANES), jnp.float32),
             pltpu.VMEM((fields, 3 * nx, ny + LANES), jnp.float32),
             pltpu.VMEM((fields, 3 * nx, ny + LANES), jnp.float32),
@@ -425,15 +472,15 @@
             pltpu.VMEM((syncs, total, 1, LANES), jnp.float32),
             pltpu.VMEM((fields, ny), jnp.float32),
             pltpu.VMEM((n_sub * n_gx, fields, ny), jnp.float32),
-            pltpu.SemaphoreType.DMA((2,)),
-            pltpu.SemaphoreType.DMA((16,)),
-            pltpu.SemaphoreType.DMA((16,)),
+            pltpu.SemaphoreType.DMA((3,)),
+            pltpu.SemaphoreType.DMA((32,)),
+            pltpu.SemaphoreType.DMA((32,)),
             pltpu.SemaphoreType.DMA((syncs,)),
             pltpu.SemaphoreType.DMA((syncs,)),
             pltpu.SemaphoreType.DMA((2,)),
         ],
         compiler_params=pltpu.CompilerParams(
-            collective_id=0, has_side_effects=True, vmem_limit_bytes=48 * 2**20),
+            collective_id=0, has_side_effects=True, vmem_limit_bytes=67043328),
     )(state, damping, weights)
 
 

time: 45.3 us -> 41.7 us (0.921)
  Pallas kernels: 40.9 us -> 38.8 us
  local copies, waits for them, and re-layouts: 3.55 us -> 2.07 us
    pallas_call x1, Pallas kernels: 40.9 us -> 38.8 us  [shards(): pl.pallas_call(functools.partial(kernel, sizes), out_shape=(jax.ShapeDtyp...]
    unnamed x8 -> x4, local copies, waits for them, and re-layouts: 3.55 us -> 2.07 us
where the time goes in v3:
time: 41.7 us; the launch traced here: 41.5 us
  Pallas kernels  38.8 us (93%)
  local copies, waits for them, and re-layouts  2.07 us (5%)
  between operations  0.65 us (2%)
    pallas_call x1, Pallas kernels, shards(): pl.pallas_call(functools.partial(kernel, sizes), out_shape=(jax.ShapeDtyp...  38.8 us
    unnamed x4, local copies, waits for them, and re-layouts  2.07 us

profile of v3, /device:TPU:0, one launch (start us, length us, event | category | flops | bytes accessed | tf_op | source)
XLA Modules:
  0.0 41.5 jit_solution(9596748235852964773)
XLA Ops:
  0.6 38.8 %shard_map.50 = (f32[4,16,256]{2,1,0:T(8,128)}, f32[4,256]{1,0:T(4,128)}) custom-call(f32[4,16,256]{2,1,0:T(8,128)} %state.1, f32[4,16,256]{2,1,0:T(8,128)} %damping.1, f32[4]{0:T(128)} %weights_in.1), custom_call_target="tpu_custom_call" | custom-call | tf_op jit(solution)/shard_map/pallas_call | solution.py:452
  39.5 0.0 copy-start
  39.5 1.5 %copy.7 = f32[4,16,256]{2,1,0:T(8,128)} copy(f32[4,16,256]{2,1,0:T(8,128)} %get-tuple-element.4) | data formatting | bytes 131072
  40.9 0.0 copy-done
  40.9 0.6 %copy.8 = f32[4,256]{1,0:T(4,128)} copy(f32[4,256]{1,0:T(4,128)S(1)} %copy-done) | data formatting | bytes 8192
Async XLA Ops:
  39.5 1.5 %copy-start = (f32[4,256]{1,0:T(4,128)S(1)}, f32[4,256]{1,0:T(4,128)}, u32[]{:S(2)}) copy-start(f32[4,256]{1,0:T(4,128)} %get-tuple-element.5) | copy-start | bytes 12292
